TPU v7x, 32 devices: a whole 2x2x4 slice. The times are simulated.
32 devices in a mesh: groups: 2 (over y), gx: 4 (over z), gy: 2 (over x), gz: 2 (over core).
Axes of the slice: x: 2, y: 2, z: 4, core: 2. Of those that a mesh axis runs over, the one named last changes fastest.
Arguments:
- pair: float32 [256, 48, 48], P(('groups', 'gz'), 'gx', 'gy'), parts along dimension 0, may hold values from -6 to 6
- residue_mask: int32 [96], P('groups'), parts along dimension 0, may hold values 0 or 1
- norm_in_gain: float32 [2, 128], P(None, 'gz'), may hold values from 0.25 to 1.75
- proj_weight: bfloat16 [2, 4, 128, 128], P(None, None, None, 'gz'), may hold values from -0.5 to 0.5
- gate_weight: bfloat16 [2, 128, 128], P(None, None, 'gz'), may hold values from -0.5 to 0.5
- norm_out_gain: float32 [2, 128], P(None, 'gz'), may hold values from 0.25 to 1.75
- out_weight: bfloat16 [2, 128, 128], P(None, None, 'gz'), may hold values from -0.5 to 0.5
Outputs:
- pair_out: float32 [256, 48, 48], P(('groups', 'gz'), 'gx', 'gy'), parts along dimension 0
There are 2 independent parts, one for each index of `groups`. A program takes and returns all parts, laid end to end along the dimension named above; an argument that names none is the same for every part. Nothing has to cross between parts.
All inputs are finite; a program needn't handle non-finite values.
Results may differ from a plain program's by a relative error of at most 0.006.
Values may be sent and summed in bfloat16 or wider, within the bound.
No kernel may reach another device: no remote copies, remote signals or barrier semaphores. Data moves between devices by JAX's collectives and lax.ppermute only.
A program may use at most 64 MiB of HBM per device.

v0:
```python
import jax
import jax.numpy as jnp
from jax import lax
from jax.sharding import PartitionSpec as P

EPSILON = 1e-05


def layer_norm_gathered(values, gain_part):
    full_values, full_gain = (
        lax.all_gather(values, "gz", axis=0, tiled=True),
        lax.all_gather(gain_part, "gz", axis=0, tiled=True),
    )
    mean_val = jnp.mean(full_values, axis=0)
    centred = full_values - mean_val
    spread = jnp.mean(centred * centred, axis=0)
    result = (centred * lax.rsqrt(spread + EPSILON) * full_gain[:, None, None]).astype(jnp.bfloat16)
    return result


def transpose_tile(pair_tile):
    depth_dim, tile_rows, tile_cols = pair_tile.shape
    across = lax.axis_size("gy")
    down_size = lax.axis_size("gx")
    quarter = tile_rows // across
    spread_rows = lax.all_to_all(pair_tile, "gy", split_axis=1, concat_axis=2, tiled=True)
    blocks = spread_rows.reshape(depth_dim, quarter, down_size, tile_rows)
    blocks = jnp.transpose(blocks, (0, 3, 2, 1))[:, :, :, None, :]
    moved_back = lax.all_to_all(
        lax.all_to_all(blocks, "gx", split_axis=2, concat_axis=2, tiled=True),
        "gy",
        split_axis=2,
        concat_axis=3,
        tiled=True,
    )
    return moved_back.reshape(depth_dim, tile_rows, tile_cols)


def fold_panels(left_tile, right_tile):
    left_panel = lax.all_gather(left_tile, "gy", axis=2, tiled=True)
    return jnp.einsum(
        "hik,hkj->hij",
        left_panel,
        lax.all_gather(right_tile, "gx", axis=1, tiled=True),
        preferred_element_type=jnp.float32,
    )


def per_device(
    pair, residue_mask, norm_in_gain, proj_weight, gate_weight, norm_out_gain, out_weight
):
    tile_rows = pair.shape[1]
    tile_cols = pair.shape[2]
    row_start = lax.axis_index("gx") * tile_rows
    col_start = lax.axis_index("gy") * tile_cols
    row_flags = lax.dynamic_slice_in_dim(residue_mask, row_start, tile_rows).astype(jnp.float32)
    col_flags = lax.dynamic_slice_in_dim(residue_mask, col_start, tile_cols).astype(jnp.float32)
    pair_mask = row_flags[:, None] * col_flags[None, :]
    current = pair
    for update in range(2):
        normed = layer_norm_gathered(current, norm_in_gain[update])
        projected = jnp.einsum(
            "cij,pch->phij", normed, proj_weight[update], preferred_element_type=jnp.float32
        )
        left_tile = (jax.nn.sigmoid(projected[0]) * projected[1] * pair_mask).astype(jnp.bfloat16)
        right_tile = (jax.nn.sigmoid(projected[2]) * projected[3] * pair_mask).astype(jnp.bfloat16)
        gate_values = jax.nn.sigmoid(
            jnp.einsum(
                "cij,cd->dij", normed, gate_weight[update], preferred_element_type=jnp.float32
            )
        )
        if update == 0:
            triangle = fold_panels(left_tile, transpose_tile(right_tile))
        else:
            triangle = fold_panels(transpose_tile(left_tile), right_tile)
        tri_normed = layer_norm_gathered(triangle, norm_out_gain[update])
        current = current + gate_values * jnp.einsum(
            "hij,hd->dij", tri_normed, out_weight[update], preferred_element_type=jnp.float32
        )
    return current


def solution(mesh):
    return jax.shard_map(
        per_device,
        mesh=mesh,
        in_specs=(
            P(("groups", "gz"), "gx", "gy"),
            P("groups"),
            P(None, "gz"),
            P(None, None, None, "gz"),
            P(None, None, "gz"),
            P(None, "gz"),
            P(None, None, "gz"),
        ),
        out_specs=P(("groups", "gz"), "gx", "gy"),
        check_vma=False,
    )
```

profile of v0, /device:TPU:0, one launch (start us, length us, event | category | flops | bytes accessed | tf_op | source)
XLA Modules:
  0.0 108.9 jit_solution(13316939528707844448)
XLA Ops:
  0.0 0.7 copy-done.7
  0.7 0.6 dynamic-slice
  1.9 0.7 copy-done.4
  2.8 0.7 copy-done.5
  3.6 1.2 %copy.59 = f32[64,12,24]{2,1,0:T(8,128)S(1)} copy(f32[64,12,24]{0,2,1:T(8,128)} %param.7) | data formatting | bytes 147456 | tf_op args[0]
  4.8 2.7 %all_gather.36 = f32[128,12,24]{2,1,0:T(8,128)S(1)} all-gather(f32[64,12,24]{2,1,0:T(8,128)S(1)} %copy.59), channel_id=1, replica_groups=mesh['groups'=2,'gx'=4,'gy'=2,'gz'=2] {'gz'}, dimensions={0}, use_global_device_ids=true | all-gather | bytes 221184 | tf_op jit(solution)/shard_map/all_gather | solution.py:11
  7.5 0.3 copy.60
  8.0 0.2 multiply_reduce_fusion.3
  8.2 0.6 copy-done.6
  9.1 2.5 %all-reduce.4 = (f32[128]{0:T(128)S(1)}, f32[128]{0:T(128)S(1)}, f32[128]{0:T(128)S(1)}, f32[128]{0:T(128)S(1)}) all-reduce(f32[128]{0:T(128)S(1)} %bitcast_dynamic-update-slice_fusion.3, f32[128]{0:T(128)S(1)} %bitcast_dynamic-update-slice_fusion.2, ...), channel_id=2, replica_groups=mesh['groups'=2,'gx'=4,'gy'=2,'gz'=2] {'gz'}, use_global_device_ids=true, to_apply=%add | all-reduce | flops 512 | bytes 4096
  11.6 0.3 convolution_bitcast_fusion.1
  12.1 7.8 %all_to_all.70 = bf16[2,2,4608]{2,1,0:T(2,128)(2,1)S(1)} all-to-all(bf16[2,2,4608]{2,1,0:T(2,128)(2,1)S(1)} %reshape.147), channel_id=1, replica_groups=mesh['groups'=2,'gx'=4,'gy'=2,'gz'=2] {'gy'}, dimensions={0} | all-to-all | bytes 73728 | tf_op jit(solution)/shard_map/all_to_all | solution.py:26
  20.2 10.3 %all_to_all.72 = bf16[4,2,2304]{2,1,0:T(2,128)(2,1)S(1)} all-to-all(bf16[4,2,2304]{2,1,0:T(2,128)(2,1)S(1)} %reshape.149), channel_id=1, replica_groups=mesh['groups'=2,'gx'=4,'gy'=2,'gz'=2] {'gx'}, dimensions={0} | all-to-all | bytes 73728 | tf_op jit(solution)/shard_map/all_to_all | solution.py:30
  30.7 0.7 reshape.151
  31.4 3.3 %all-to-all-start.2 = ((bf16[2,2,4608]{2,1,0:T(2,128)(2,1)}), bf16[2,2,4608]{2,1,0:T(2,128)(2,1)S(1)}, u32[]{:S(2)}, u32[]{:S(2)}) async-start(bf16[2,2,4608]{2,1,0:T(2,128)(2,1)} %reshape.151), calls=%async_computation.2 | async-start | bytes 73728 | tf_op jit(solution)/shard_map/all_to_all | solution.py:29
  34.7 5.0 %all_gather.38 = bf16[64,12,48]{0,2,1:T(8,128)(2,1)S(1)} all-gather(bf16[64,12,24]{0,2,1:T(8,128)(2,1)S(1)} %get-tuple-element.12), channel_id=1, replica_groups=mesh['groups'=2,'gx'=4,'gy'=2,'gz'=2] {'gy'}, dimensions={2}, use_global_device_ids=true | all-gather | bytes 110592 | tf_op jit(solution)/shard_map/all_gather | solution.py:40
  39.7 0.3 copy.69
  40.2 13.9 %all_gather.39 = bf16[64,48,24]{0,2,1:T(8,128)(2,1)S(1)} all-gather(bf16[64,12,24]{0,2,1:T(8,128)(2,1)S(1)} %reshape.104), channel_id=1, replica_groups=mesh['groups'=2,'gx'=4,'gy'=2,'gz'=2] {'gx'}, dimensions={1}, use_global_device_ids=true | all-gather | bytes 184320 | tf_op jit(solution)/shard_map/all_gather | solution.py:44
  54.1 0.6 copy.70
  54.8 0.3 fusion.62
  55.1 2.5 %all_gather.40 = f32[128,12,24]{2,1,0:T(8,128)S(1)} all-gather(f32[64,12,24]{2,1,0:T(8,128)S(1)} %fusion.62), channel_id=1, replica_groups=mesh['groups'=2,'gx'=4,'gy'=2,'gz'=2] {'gz'}, dimensions={0}, use_global_device_ids=true | all-gather | bytes 221184 | tf_op jit(solution)/shard_map/all_gather | solution.py:11
  57.7 0.3 copy.71
  58.0 0.1 reduce_sum.74
  58.1 0.2 multiply_reduce_fusion.2
  58.4 0.5 copy-done.2
  58.9 0.3 fusion.40
  59.2 0.6 copy-done
  59.8 0.3 fusion.6
  60.1 0.3 copy.72
  60.4 2.6 %all_gather.42 = f32[128,12,24]{2,1,0:T(8,128)S(1)} all-gather(f32[64,12,24]{2,1,0:T(8,128)S(1)} %copy.72), channel_id=1, replica_groups=mesh['groups'=2,'gx'=4,'gy'=2,'gz'=2] {'gz'}, dimensions={0}, use_global_device_ids=true | all-gather | bytes 221184 | tf_op jit(solution)/shard_map/all_gather | solution.py:11
  62.9 0.3 copy.73
  63.4 0.2 multiply_reduce_fusion.1
  63.6 0.3 convolution_bitcast_fusion
  64.2 7.3 %all_to_all.71 = bf16[2,2,4608]{2,1,0:T(2,128)(2,1)S(1)} all-to-all(bf16[2,2,4608]{2,1,0:T(2,128)(2,1)S(1)} %reshape.153), channel_id=1, replica_groups=mesh['groups'=2,'gx'=4,'gy'=2,'gz'=2] {'gy'}, dimensions={0} | all-to-all | bytes 73728 | tf_op jit(solution)/shard_map/all_to_all | solution.py:26
  71.8 8.0 %all_to_all.73 = bf16[4,2,2304]{2,1,0:T(2,128)(2,1)S(1)} all-to-all(bf16[4,2,2304]{2,1,0:T(2,128)(2,1)S(1)} %reshape.155), channel_id=1, replica_groups=mesh['groups'=2,'gx'=4,'gy'=2,'gz'=2] {'gx'}, dimensions={0} | all-to-all | bytes 73728 | tf_op jit(solution)/shard_map/all_to_all | solution.py:30
  80.0 0.7 reshape.157
  80.7 3.3 %all-to-all-start.5 = ((bf16[2,2,4608]{2,1,0:T(2,128)(2,1)}), bf16[2,2,4608]{2,1,0:T(2,128)(2,1)S(1)}, u32[]{:S(2)}, u32[]{:S(2)}) async-start(bf16[2,2,4608]{2,1,0:T(2,128)(2,1)} %reshape.157), calls=%async_computation.5 | async-start | bytes 73728 | tf_op jit(solution)/shard_map/all_to_all | solution.py:29
  84.0 14.0 %all_gather.45 = bf16[64,48,24]{0,2,1:T(8,128)(2,1)S(1)} all-gather(bf16[64,12,24]{0,2,1:T(8,128)(2,1)S(1)} %get-tuple-element.9), channel_id=1, replica_groups=mesh['groups'=2,'gx'=4,'gy'=2,'gz'=2] {'gx'}, dimensions={1}, use_global_device_ids=true | all-gather | bytes 184320 | tf_op jit(solution)/shard_map/all_gather | solution.py:44
  98.0 0.6 copy.80
  98.8 5.0 %all_gather.44 = bf16[64,12,48]{0,2,1:T(8,128)(2,1)S(1)} all-gather(bf16[64,12,24]{0,2,1:T(8,128)(2,1)S(1)} %reshape.106), channel_id=1, replica_groups=mesh['groups'=2,'gx'=4,'gy'=2,'gz'=2] {'gy'}, dimensions={2}, use_global_device_ids=true | all-gather | bytes 110592 | tf_op jit(solution)/shard_map/all_gather | solution.py:40
  103.9 0.3 copy.79
  104.1 0.3 fusion.63
  104.5 2.5 %all_gather.46 = f32[128,12,24]{2,1,0:T(8,128)S(1)} all-gather(f32[64,12,24]{2,1,0:T(8,128)S(1)} %fusion.63), channel_id=1, replica_groups=mesh['groups'=2,'gx'=4,'gy'=2,'gz'=2] {'gz'}, dimensions={0}, use_global_device_ids=true | all-gather | bytes 221184 | tf_op jit(solution)/shard_map/all_gather | solution.py:11
  107.0 0.3 copy.81
  107.3 0.1 reduce_sum.78
  107.5 0.2 multiply_reduce_fusion
  107.7 0.3 fusion.41
  108.0 1.0 fusion.11
  (59 shorter events, 2.7 us)
Async XLA Ops:
  0.0 0.7 copy-start.7
  1.9 0.7 copy-start.4
  2.8 0.7 copy-start.5
  7.9 3.6 %copy-start.1 = (bf16[2,4,128,64]{2,3,1,0:T(8,128)(2,1)S(1)}, bf16[2,4,128,64]{2,3,1,0:T(8,128)(2,1)}, u32[]{:S(2)}) copy-start(bf16[2,4,128,64]{2,3,1,0:T(8,128)(2,1)} %param.10) | copy-start | bytes 393220
  8.2 0.7 copy-start.6
  31.4 8.6 %all-to-all-start.2 = ((bf16[2,2,4608]{2,1,0:T(2,128)(2,1)}), bf16[2,2,4608]{2,1,0:T(2,128)(2,1)S(1)}, u32[]{:S(2)}, u32[]{:S(2)}) async-start(bf16[2,2,4608]{2,1,0:T(2,128)(2,1)} %reshape.151), calls=%async_computation.2 | async-start | bytes 73728 | tf_op jit(solution)/shard_map/all_to_all | solution.py:29
  58.1 0.8 copy-start.2
  58.9 0.9 copy-start
  58.9 0.9 copy-start.3
  80.7 17.9 %all-to-all-start.5 = ((bf16[2,2,4608]{2,1,0:T(2,128)(2,1)}), bf16[2,2,4608]{2,1,0:T(2,128)(2,1)S(1)}, u32[]{:S(2)}, u32[]{:S(2)}) async-start(bf16[2,2,4608]{2,1,0:T(2,128)(2,1)} %reshape.157), calls=%async_computation.5 | async-start | bytes 73728 | tf_op jit(solution)/shard_map/all_to_all | solution.py:29
where the time goes:
time: 110 us; the launch traced here: 109 us
  blocking collectives  84.3 us (77%)
  local copies, waits for them, and re-layouts  12.3 us (11%)
  starting transfers between devices  6.52 us (6%)
  matrix products  3.03 us (3%)
  other arithmetic  1.82 us (2%)
    all_gather x2, blocking collectives, fold_panels(): lax.all_gather(right_tile, 'gx', axis=1, tiled=True)  27.9 us
    all_to_all x2, blocking collectives, transpose_tile(): lax.all_to_all(blocks, 'gx', split_axis=2, concat_axis=2, tiled=True)  18.4 us
    all_to_all x2, blocking collectives, transpose_tile(): lax.all_to_all(pair_tile, 'gy', split_axis=1, concat_axis=2, tiled=True)  15.2 us
    all_gather x4, blocking collectives, layer_norm_gathered(): lax.all_gather(values, 'gz', axis=0, tiled=True)  10.3 us
    all_gather x2, blocking collectives, fold_panels(): left_panel = lax.all_gather(left_tile, 'gy', axis=2, tiled=True)  10 us
    unnamed x42, local copies, waits for them, and re-layouts  8.64 us
    all_to_all x2, starting transfers between devices, transpose_tile(): lax.all_to_all(lax.all_to_all(blocks, 'gx', split_axis=2, concat_axis=2,...  6.52 us
    unnamed x1, blocking collectives  2.48 us
  transfers between devices with their start and end apart: 2, of which 0 were waited for; matrix products, arithmetic and copies ran while one was open for 1% of the time, Pallas kernels for 0%

commit v1 on v0

--- a/solution.py
+++ b/solution.py
@@ -1,9 +1,270 @@
+import functools
+
 import jax
 import jax.numpy as jnp
 from jax import lax
+from jax.experimental import pallas as pl
+from jax.experimental.pallas import tpu as pltpu
 from jax.sharding import PartitionSpec as P
 
 EPSILON = 1e-05
+F32 = jnp.float32
+BF16 = jnp.bfloat16
+REPLICATED_LIMIT = 4 * 1024 * 1024
+
+
+def sigmoid(x):
+    return 0.5 * jnp.tanh(0.5 * x) + 0.5
+
+
+def lane_norm(x, gain):
+    mean = jnp.mean(x, axis=-1, keepdims=True)
+    d = x - mean
+    var = jnp.mean(d * d, axis=-1, keepdims=True)
+    return d * lax.rsqrt(var + EPSILON) * gain
+
+
+def dot(x, w):
+    return jnp.dot(x.astype(BF16), w, preferred_element_type=F32)
+
+
+def centre_kernel(own, other, out, *, half):
+    core = lax.axis_index("gz")
+    part, rows, cols = own.shape
+    total = jnp.sum(own[...], axis=0) + jnp.sum(other[...], axis=0)
+    mean = total * (1.0 / (2 * part))
+
+    def emit(first, second, base):
+        pieces = []
+        for q in range(half):
+            i = base + q
+            both = jnp.concatenate([first[:, i, :], second[:, i, :]], axis=0)
+            pieces.append(jnp.transpose(both - mean[i : i + 1, :]))
+        out[...] = jnp.concatenate(pieces, axis=0).astype(BF16)
+
+    @pl.when(core == 0)
+    def _():
+        emit(own, other, 0)
+
+    @pl.when(core == 1)
+    def _():
+        emit(other, own, half)
+
+
+def main_kernel(
+    own, other, mask, gain_in, gain_out, wleft, wright, wgate, wout, pair, out,
+    raw, normed, left, rightt, tri, first_update, znext, right1, left1, total,
+    *, res, tile_rows, tile_cols, grid_rows, grid_cols,
+):
+    ch = mask.shape[1]
+    half = tile_rows // 2
+    ipad = -(-tile_rows // 8) * 8
+    span = tile_cols + ipad
+    row_block = lax.axis_index("gx")
+    col_block = lax.axis_index("gy")
+    core = lax.axis_index("gz")
+    mk = mask[:res, :]
+
+    for source, which in ((own, core), (other, 1 - core)):
+
+        def norm_block(block, carry, source=source, which=which):
+            x = source[block].astype(F32)
+            var = jnp.mean(x * x, axis=-1, keepdims=True)
+            zn = x * lax.rsqrt(var + EPSILON) * gain_in[0:1, :]
+            base = (block // grid_cols * tile_rows + which * half) * res + block % grid_cols * tile_cols
+            for q in range(half):
+                at = pl.ds(pl.multiple_of(base + q * res, 8), tile_cols)
+                raw[at, :] = x[q * tile_cols : (q + 1) * tile_cols]
+                normed[at, :] = zn[q * tile_cols : (q + 1) * tile_cols]
+            return carry
+
+        lax.fori_loop(0, grid_rows * grid_cols, norm_block, 0)
+    raw[pl.ds(res * res, 8), :] = jnp.zeros((8, ch), F32)
+    normed[pl.ds(res * res, 8), :] = jnp.zeros((8, ch), F32)
+
+    def gated(x, w):
+        p = dot(x, w)
+        return sigmoid(p[:, :ch]) * p[:, ch:]
+
+    step = 8
+
+    def left_block(block, carry):
+        at = pl.ds(pl.multiple_of(block * step * res, 8), step * res)
+        y = gated(normed[at, :], wleft[0]).reshape(step, res, ch)
+        rows = mask[pl.ds(pl.multiple_of(block * step, 8), step), :]
+        y = y * mk[None] * rows[:, None, :]
+        left[at, :] = y.reshape(step * res, ch)
+        return carry
+
+    lax.fori_loop(0, res // step, left_block, 0)
+
+    rightt[...] = jnp.zeros_like(rightt)
+    group = 4
+
+    def right_rows(first, slot, count):
+        def block(n, carry):
+            x = normed[pl.ds(pl.multiple_of((first + n * group) * res, 8), group * res), :]
+            y = gated(x, wright[0])
+            for q in range(group):
+                row = mask[pl.ds(first + n * group + q, 1), :]
+                v = y[q * res : (q + 1) * res] * mk * row
+                rightt[pl.ds(slot + n * group + q, res, stride=span), :] = v
+            return carry
+
+        lax.fori_loop(0, count // group, block, 0)
+
+    right_rows(col_block * tile_cols, 0, tile_cols)
+    right_rows(row_block * tile_rows, tile_cols, tile_rows)
+
+    block_rows = 4
+
+    def tri_block(n, carry):
+        accs = [jnp.zeros((span, ch), F32) for _ in range(block_rows)]
+        for k in range(res):
+            r = rightt[k * span : (k + 1) * span, :]
+            for q in range(block_rows):
+                accs[q] = accs[q] + left[pl.ds((n * block_rows + q) * res + k, 1), :] * r
+        for q in range(block_rows):
+            at = pl.ds(pl.multiple_of((n * block_rows + q) * span, 8), span)
+            tri[at, :] = lane_norm(accs[q], gain_out[0:1, :])
+        return carry
+
+    lax.fori_loop(0, res // block_rows, tri_block, 0)
+
+    wide = 8
+
+    def out_block(n, carry):
+        zs, ns = [], []
+        for q in range(wide):
+            r = n * wide + q
+            at_cols = pl.ds(pl.multiple_of(r * res + col_block * tile_cols, 8), tile_cols)
+            at_rows = pl.ds(r * res + row_block * tile_rows, ipad)
+            zs += [raw[at_cols, :], raw[at_rows, :]]
+            ns += [normed[at_cols, :], normed[at_rows, :]]
+        at = pl.ds(pl.multiple_of(n * wide * span, 8), wide * span)
+        gate = sigmoid(dot(jnp.concatenate(ns, axis=0), wgate[0]))
+        update = gate * dot(tri[at, :], wout[0])
+        first_update[at, :] = update
+        znext[at, :] = lane_norm(jnp.concatenate(zs, axis=0) + update, gain_in[1:2, :])
+        return carry
+
+    lax.fori_loop(0, res // wide, out_block, 0)
+
+    def second_block(n, carry):
+        rs, ls = [], []
+        for q in range(wide):
+            at = (n * wide + q) * span
+            rs.append(znext[pl.ds(pl.multiple_of(at, 8), tile_cols), :])
+            ls.append(znext[pl.ds(pl.multiple_of(at + tile_cols, 8), ipad), :])
+        rows = mask[pl.ds(pl.multiple_of(n * wide, 8), wide), :][:, None, :]
+        cmask = mask[pl.ds(pl.multiple_of(col_block * tile_cols, 8), tile_cols), :]
+        imask = mask[pl.ds(row_block * tile_rows, ipad), :]
+        r = gated(jnp.concatenate(rs, axis=0), wright[1]).reshape(wide, tile_cols, ch)
+        r = r * rows * cmask[None]
+        right1[pl.ds(pl.multiple_of(n * wide * tile_cols, 8), wide * tile_cols), :] = r.reshape(wide * tile_cols, ch)
+        v = gated(jnp.concatenate(ls, axis=0), wleft[1]).reshape(wide, ipad, ch)
+        v = v * rows * imask[None]
+        left1[pl.ds(pl.multiple_of(n * wide * ipad, 8), wide * ipad), :] = v.reshape(wide * ipad, ch)
+        return carry
+
+    lax.fori_loop(0, res // wide, second_block, 0)
+
+    def tri1_block(k, accs):
+        r = right1[pl.ds(pl.multiple_of(k * tile_cols, 8), tile_cols), :]
+        return tuple(
+            acc + left1[pl.ds(k * ipad + i, 1), :] * r for i, acc in enumerate(accs)
+        )
+
+    accs = lax.fori_loop(
+        0, res, tri1_block, tuple(jnp.zeros((tile_cols, ch), F32) for _ in range(tile_rows)), unroll=4
+    )
+    tn = jnp.concatenate([lane_norm(acc, gain_out[1:2, :]) for acc in accs], axis=0)
+    ns, us = [], []
+    for i in range(tile_rows):
+        at = pl.ds(pl.multiple_of((row_block * tile_rows + i) * span, 8), tile_cols)
+        ns.append(znext[at, :])
+        us.append(first_update[at, :])
+    gate = sigmoid(dot(jnp.concatenate(ns, axis=0), wgate[1]))
+    total[...] = jnp.concatenate(us, axis=0) + gate * dot(tn, wout[1])
+    part = ch // 2
+    for i in range(tile_rows):
+        t = pltpu.roll(total[i * tile_cols : (i + 1) * tile_cols, :], core * part, 1)
+        out[:, i, :] = pair[:, i, :] + jnp.transpose(t)[:part]
+
+
+def swap_cores(x):
+    return lax.ppermute(x, "gz", [(0, 1), (1, 0)])
+
+
+def join_cores(own, other, axis):
+    first = jnp.concatenate([own, other], axis=axis)
+    second = jnp.concatenate([other, own], axis=axis)
+    return jnp.where(lax.axis_index("gz") == 0, first, second)
+
+
+def replicated(
+    pair, residue_mask, norm_in_gain, proj_weight, gate_weight, norm_out_gain, out_weight
+):
+    part, tile_rows, tile_cols = pair.shape
+    grid_rows, grid_cols = lax.axis_size("gx"), lax.axis_size("gy")
+    res = residue_mask.shape[0]
+    ch = 2 * part
+    half = tile_rows // 2
+    ipad = -(-tile_rows // 8) * 8
+    span = tile_cols + ipad
+
+    own_weights = jnp.concatenate(
+        [proj_weight, gate_weight[:, None], out_weight[:, None]], axis=1
+    )
+    own_gains = jnp.concatenate([norm_in_gain, norm_out_gain], axis=0)
+    other_pair = swap_cores(pair)
+    weights = join_cores(own_weights, swap_cores(own_weights), 3)
+    gains = join_cores(own_gains, swap_cores(own_gains), 1)
+
+    message = pl.pallas_call(
+        functools.partial(centre_kernel, half=half),
+        out_shape=jax.ShapeDtypeStruct((half * tile_cols, ch), BF16),
+        name="centre",
+    )(pair, other_pair)
+    chips = grid_rows * grid_cols
+    gathered = lax.all_to_all(
+        jnp.broadcast_to(message[None], (chips,) + message.shape), ("gx", "gy"), 0, 0
+    )
+    other_gathered = swap_cores(gathered)
+
+    wleft = jnp.concatenate([weights[:, 0], weights[:, 1]], axis=2)
+    wright = jnp.concatenate([weights[:, 2], weights[:, 3]], axis=2)
+    mask = jnp.pad(residue_mask.astype(F32), (0, 8))
+    mask = jnp.broadcast_to(mask[:, None], (res + 8, ch))
+    vmem = lambda rows: pltpu.VMEM((rows, ch), F32)
+    return pl.pallas_call(
+        functools.partial(
+            main_kernel,
+            res=res,
+            tile_rows=tile_rows,
+            tile_cols=tile_cols,
+            grid_rows=grid_rows,
+            grid_cols=grid_cols,
+        ),
+        out_shape=jax.ShapeDtypeStruct(pair.shape, F32),
+        scratch_shapes=[
+            vmem(res * res + 8),
+            vmem(res * res + 8),
+            vmem(res * res),
+            vmem(res * span),
+            vmem(res * span),
+            vmem(res * span),
+            vmem(res * span),
+            vmem(res * tile_cols),
+            vmem(res * ipad),
+            vmem(tile_rows * tile_cols),
+        ],
+        compiler_params=pltpu.CompilerParams(vmem_limit_bytes=48 * 1024 * 1024),
+        name="update",
+    )(
+        gathered, other_gathered, mask, gains[:2], gains[2:], wleft, wright,
+        weights[:, 4], weights[:, 5], pair,
+    )
 
 
 def layer_norm_gathered(values, gain_part):
@@ -46,7 +307,7 @@
     )
 
 
-def per_device(
+def distributed(
     pair, residue_mask, norm_in_gain, proj_weight, gate_weight, norm_out_gain, out_weight
 ):
     tile_rows = pair.shape[1]
@@ -80,6 +341,23 @@
     return current
 
 
+def fits_replicated(pair, residue_mask):
+    part, tile_rows, tile_cols = pair.shape
+    res = residue_mask.shape[0]
+    return (
+        lax.axis_size("gz") == 2
+        and res * res * part * 2 * 4 <= REPLICATED_LIMIT
+        and res % 8 == 0
+        and tile_rows % 4 == 0
+        and tile_cols % 8 == 0
+    )
+
+
+def per_device(pair, residue_mask, *parameters):
+    plan = replicated if fits_replicated(pair, residue_mask) else distributed
+    return plan(pair, residue_mask, *parameters)
+
+
 def solution(mesh):
     return jax.shard_map(
         per_device,

time: 110 us -> 43.2 us (0.39)
  blocking collectives: 84.3 us -> 0 us
  Pallas kernels: 0 us -> 17.6 us
  waiting for transfers between devices: 0.01 us -> 10.9 us
  local copies, waits for them, and re-layouts: 12.3 us -> 5.68 us
  matrix products: 3.03 us -> 0 us
  starting transfers between devices: 6.52 us -> 7.91 us
  other arithmetic: 1.82 us -> 0.65 us
    all_gather x8 -> x0, blocking collectives: 48.2 us -> none  [the longest x2 27.9 us: fold_panels(): lax.all_gather(right_tile, 'gx', axis=1, tiled=True)]
    all_to_all x4 -> x0, blocking collectives: 33.6 us -> none  [the longest x2 18.4 us: transpose_tile(): lax.all_to_all(blocks, 'gx', split_axis=2, concat_axis=2, tiled=True)]
    pallas_call x0 -> x2, Pallas kernels: none -> 17.6 us  [the longest x1 15.4 us: replicated(): pl.pallas_call(functools.partial(main_kernel, res=res, tile_rows=tile_row...]
    all_to_all x2 -> x1, waiting for transfers between devices: 0.01 us -> 7.55 us  [replicated(): lax.all_to_all(jnp.broadcast_to(message[None], (chips,) + message.shape),...]
    unnamed x42 -> x22, local copies, waits for them, and re-layouts: 8.64 us -> 3.2 us
    ppermute x0 -> x4, waiting for transfers between devices: none -> 3.35 us  [swap_cores(): return lax.ppermute(x, 'gz', [(0, 1), (1, 0)])]
    all_gather x8 -> x0, local copies, waits for them, and re-layouts: 3.05 us -> none  [the longest x4 1.32 us: layer_norm_gathered(): lax.all_gather(values, 'gz', axis=0, tiled=True)]
    dot_general x8 -> x0, matrix products: 3.03 us -> none  [the longest x2 1.25 us: per_device(): jnp.einsum('cij,cd->dij', normed, gate_weight[update], preferred_element_...]
  transfers between devices with their start and end apart: 2 -> 5, of which waited for: 0 -> 4; matrix products, arithmetic and copies ran while one was open for 1% -> 6% of each run, Pallas kernels for 0% -> 5%
where the time goes in v1:
time: 43.2 us; the launch traced here: 42.9 us
  Pallas kernels  17.6 us (41%)
  waiting for transfers between devices  10.9 us (25%)
  starting transfers between devices  7.91 us (18%)
  local copies, waits for them, and re-layouts  5.68 us (13%)
  other arithmetic  0.65 us (2%)
    pallas_call x1, Pallas kernels, replicated(): pl.pallas_call(functools.partial(main_kernel, res=res, tile_rows=tile_row...  15.4 us
    all_to_all x1, waiting for transfers between devices, replicated(): lax.all_to_all(jnp.broadcast_to(message[None], (chips,) + message.shape),...  7.55 us
    all_to_all x1, starting transfers between devices, replicated(): lax.all_to_all(jnp.broadcast_to(message[None], (chips,) + message.shape),...  7.16 us
    ppermute x4, waiting for transfers between devices, swap_cores(): return lax.ppermute(x, 'gz', [(0, 1), (1, 0)])  3.35 us
    unnamed x22, local copies, waits for them, and re-layouts  3.2 us
    pallas_call x1, Pallas kernels, replicated(): pl.pallas_call(functools.partial(centre_kernel, half=half), out_shape=jax...  2.17 us
    broadcast_in_dim x1, local copies, waits for them, and re-layouts, replicated(): jnp.broadcast_to(message[None], (chips,) + message.shape)  1.51 us
  transfers between devices with their start and end apart: 5, of which 4 were waited for; matrix products, arithmetic and copies ran while one was open for 6% of the time, Pallas kernels for 5%

profile of v1, /device:TPU:0, one launch (start us, length us, event | category | flops | bytes accessed | tf_op | source)
XLA Modules:
  0.0 42.9 jit_solution(8010236058812058108)
XLA Ops:
  0.0 0.0 copy-start.6
  0.0 0.0 copy-start.7
  0.0 0.0 copy-start.4
  0.0 0.0 copy-start.5
  0.0 1.2 %copy.9.own.pair = f32[64,12,24]{2,1,0:T(8,128)S(1)} copy(f32[64,12,24]{0,2,1:T(8,128)} %param.7) | data formatting | bytes 147456 | tf_op args[0]
  1.2 0.0 copy-start
  1.2 0.0 copy-start.3
  1.3 0.6 %collective-permute-start = (f32[64,12,24]{2,1,0:T(8,128)S(1)}, f32[64,12,24]{2,1,0:T(8,128)S(1)}, u32[]{:S(2)}, u32[]{:S(2)}) collective-permute-start(f32[64,12,24]{2,1,0:T(8,128)S(1)} %copy.9.own.pair), channel_id=1, source_target_pairs={{0,1},{1,0},{2,3},{3,2},{4,5},{5,4},{6,7},{7,6},{8,9},{9,8},{10,11... | collective-permute-start | bytes 221192 | tf_op jit(solution)/shard_map/ppermute | solution.py:196
  1.8 0.0 copy-done.6
  1.8 0.0 copy-done.7
  1.9 0.1 collective-permute-start.2
  1.9 0.0 copy-done.4
  2.0 0.1 copy.10
  2.1 0.0 copy-done.5
  2.1 0.1 copy.11
  2.2 0.1 copy-done.3
  2.3 0.2 copy.12
  2.5 0.9 %collective-permute-done.other = f32[64,12,24]{2,1,0:T(8,128)S(1)} collective-permute-done((f32[64,12,24]{2,1,0:T(8,128)S(1)}, f32[64,12,24]{2,1,0:T(8,128)S(1)}, u32[]{:S(2)}, u32[]{:S(2)}) %collective-permute-start) | collective-permute-done | bytes 73760 | tf_op jit(solution)/shard_map/ppermute | solution.py:196
  3.4 0.0 copy-done
  3.4 0.0 copy-start.2
  3.4 0.8 %copy-done.2 = f32[64,12,24]{2,1,0:T(8,128)} copy-done((f32[64,12,24]{2,1,0:T(8,128)}, f32[64,12,24]{2,1,0:T(8,128)S(1)}, u32[]{:S(2)}) %copy-start.2) | copy-done | bytes 73752
  4.2 2.2 %centre.1 = bf16[144,128]{1,0:T(8,128)(2,1)} custom-call(f32[64,12,24]{2,1,0:T(8,128)} %copy-done, f32[64,12,24]{2,1,0:T(8,128)} %copy-done.2), custom_call_target="tpu_custom_call" | custom-call | tf_op jit(solution)/shard_map/centre/pallas_call | solution.py:224
  6.3 1.5 %broadcast_in_dim.8 = bf16[8,144,128]{2,1,0:T(8,128)(2,1)} broadcast(bf16[144,128]{1,0:T(8,128)(2,1)} %centre.1), dimensions={1,2} | broadcast | bytes 331776 | tf_op jit(solution)/shard_map/broadcast_in_dim | solution.py:231
  7.9 7.2 %all-to-all-start = ((bf16[8,144,128]{2,1,0:T(8,128)(2,1)}), bf16[8,144,128]{2,1,0:T(8,128)(2,1)S(1)}, u32[]{:S(2)}, u32[]{:S(2)}) async-start(bf16[8,144,128]{2,1,0:T(8,128)(2,1)} %broadcast_in_dim.8), calls=%async_computation | async-start | bytes 589824 | tf_op jit(solution)/shard_map/all_to_all | solution.py:230
  15.0 0.1 pad_maximum_fusion
  15.1 0.1 collective-permute-start.3
  15.2 0.0 copy-start.8
  15.2 0.6 %copy-done.8 = s32[48]{0:T(128)S(1)} copy-done((s32[48]{0:T(128)S(1)}, s32[48]{0:T(128)}, u32[]{:S(2)}) %copy-start.8) | copy-done | bytes 216
  15.9 0.0 collective-permute-done.2
  15.9 0.1 maximum_select_fusion.1
  16.0 0.9 %collective-permute-done.3 = bf16[2,6,128,64]{3,2,0,1:T(8,128)(2,1)S(1)} collective-permute-done((bf16[2,6,128,64]{3,2,0,1:T(8,128)(2,1)S(1)}, bf16[2,6,128,64]{3,2,0,1:T(8,128)(2,1)S(1)}, u32[]{:S(2)}, u32[]{:S(2)}) %collective-permute-start.3) | collective-permute-done | bytes 196640 | tf_op jit(solution)/shard_map/ppermute | solution.py:196
  16.9 0.4 %maximum_select_fusion = bf16[2,6,128,128]{3,2,0,1:T(8,128)(2,1)S(1)} fusion(bf16[2,6,128,64]{3,2,0,1:T(8,128)(2,1)S(1)} %collective-permute-done.3, bf16[2,1,128,64]{3,2,0,1:T(8,128)(2,1)S(1)} %bitcast.17, bf16[2,1,128,64]{3,2,0,1:T(8,128)(2,1)S(1)} %bitcast.15, bf16[2,4,128,64]{3,2,0,1:T(8,128)(2,1)S(1)} %copy.12, pred[]{:T(512)S(6)} %eq.4), kind=kLoop, calls=%fused_computation.1 | loop fusion | flops 3342336 | bytes 786433 | tf_op jit(solution)/shard_map/jit(_where)/select_n | solution.py:202
  17.3 0.0 copy-start.1
  17.4 7.6 %all-to-all-done.own = bf16[8,144,128]{2,1,0:T(8,128)(2,1)S(1)} async-done(((bf16[8,144,128]{2,1,0:T(8,128)(2,1)}), bf16[8,144,128]{2,1,0:T(8,128)(2,1)S(1)}, u32[]{:S(2)}, u32[]{:S(2)}) %all-to-all-start) | async-done | bytes 294944 | tf_op jit(solution)/shard_map/all_to_all | solution.py:230
  24.9 0.0 collective-permute-start.1
  25.0 1.5 %collective-permute-done.1.other = bf16[8,144,128]{2,1,0:T(8,128)(2,1)S(1)} collective-permute-done((bf16[8,144,128]{2,1,0:T(8,128)(2,1)S(1)}, bf16[8,144,128]{2,1,0:T(8,128)(2,1)S(1)}, u32[]{:S(2)}, u32[]{:S(2)}) %collective-permute-start.1) | collective-permute-done | bytes 294944 | tf_op jit(solution)/shard_map/ppermute | solution.py:196
  26.5 0.1 broadcast_in_dim.9.mask
  26.6 0.0 copy-done.1
  26.6 15.4 %update.1 = f32[64,12,24]{2,1,0:T(8,128)S(1)} custom-call(bf16[8,144,128]{2,1,0:T(8,128)(2,1)S(1)} %all-to-all-done.own, bf16[8,144,128]{2,1,0:T(8,128)(2,1)S(1)} %collective-permute-done.1.other, f32[56,128]{1,0:T(8,128)S(1)} %broadcast_in_dim.9.mask, f32[2,128]{1,0:T(2,128)S(1)} %get-tuple-element.12.gain_in, f32[2,128]{1,0:T(2,128)S(1)} %get-tuple-element.11.gain_out, ...), custom_call_target="tpu_custom_call" | custom-call | tf_op jit(solution)/shard_map/update/pallas_call | solution.py:240
  42.0 0.9 %copy.14 = f32[64,12,24]{0,2,1:T(8,128)} copy(f32[64,12,24]{2,1,0:T(8,128)S(1)} %update.1) | data formatting | bytes 147456 | tf_op jit(solution)/shard_map/update/pallas_call | solution.py:240
  (6 shorter events, 0.1 us)
Async XLA Ops:
  0.0 1.8 %copy-start.6 = (f32[2,64]{1,0:T(2,128)S(1)}, f32[2,64]{1,0:T(2,128)}, u32[]{:S(2)}) copy-start(f32[2,64]{1,0:T(2,128)} %param.12) | copy-start | bytes 1540
  0.0 1.8 %copy-start.7 = (f32[2,64]{1,0:T(2,128)S(1)}, f32[2,64]{1,0:T(2,128)}, u32[]{:S(2)}) copy-start(f32[2,64]{1,0:T(2,128)} %param.9) | copy-start | bytes 1540
  0.0 1.9 %copy-start.4 = (bf16[2,128,64]{1,2,0:T(8,128)(2,1)S(1)}, bf16[2,128,64]{1,2,0:T(8,128)(2,1)}, u32[]{:S(2)}) copy-start(bf16[2,128,64]{1,2,0:T(8,128)(2,1)} %param.11) | copy-start | bytes 98308
  0.0 2.1 %copy-start.5 = (bf16[2,128,64]{1,2,0:T(8,128)(2,1)S(1)}, bf16[2,128,64]{1,2,0:T(8,128)(2,1)}, u32[]{:S(2)}) copy-start(bf16[2,128,64]{1,2,0:T(8,128)(2,1)} %param.13) | copy-start | bytes 98308
  1.2 2.1 %copy-start = (f32[64,12,24]{2,1,0:T(8,128)}, f32[64,12,24]{2,1,0:T(8,128)S(1)}, u32[]{:S(2)}) copy-start(f32[64,12,24]{2,1,0:T(8,128)S(1)} %copy.9.own.pair) | copy-start | bytes 221188
  1.2 1.0 %copy-start.3 = (bf16[2,4,128,64]{2,3,1,0:T(8,128)(2,1)S(1)}, bf16[2,4,128,64]{2,3,1,0:T(8,128)(2,1)}, u32[]{:S(2)}) copy-start(bf16[2,4,128,64]{2,3,1,0:T(8,128)(2,1)} %param.10) | copy-start | bytes 393220
  1.3 2.1 %collective-permute-start = (f32[64,12,24]{2,1,0:T(8,128)S(1)}, f32[64,12,24]{2,1,0:T(8,128)S(1)}, u32[]{:S(2)}, u32[]{:S(2)}) collective-permute-start(f32[64,12,24]{2,1,0:T(8,128)S(1)} %copy.9.own.pair), channel_id=1, source_target_pairs={{0,1},{1,0},{2,3},{3,2},{4,5},{5,4},{6,7},{7,6},{8,9},{9,8},{10,11... | collective-permute-start | bytes 221192 | tf_op jit(solution)/shard_map/ppermute | solution.py:196
  1.9 14.0 %collective-permute-start.2 = (f32[4,64]{1,0:T(4,128)S(1)}, f32[4,64]{1,0:T(4,128)S(1)}, u32[]{:S(2)}, u32[]{:S(2)}) collective-permute-start(f32[4,64]{1,0:T(4,128)S(1)} %pad_maximum_fusion.3), channel_id=1, source_target_pairs={{0,1},{1,0},{2,3},{3,2},{4,5},{5,4},{6,7},{7,6},{8,9},{9,8},{10,11... | collective-permute-start | bytes 3080 | tf_op jit(solution)/shard_map/ppermute | solution.py:196
  3.4 0.8 %copy-start.2 = (f32[64,12,24]{2,1,0:T(8,128)}, f32[64,12,24]{2,1,0:T(8,128)S(1)}, u32[]{:S(2)}) copy-start(f32[64,12,24]{2,1,0:T(8,128)S(1)} %collective-permute-done.other) | copy-start | bytes 221188
  7.9 17.0 %all-to-all-start = ((bf16[8,144,128]{2,1,0:T(8,128)(2,1)}), bf16[8,144,128]{2,1,0:T(8,128)(2,1)S(1)}, u32[]{:S(2)}, u32[]{:S(2)}) async-start(bf16[8,144,128]{2,1,0:T(8,128)(2,1)} %broadcast_in_dim.8), calls=%async_computation | async-start | bytes 589824 | tf_op jit(solution)/shard_map/all_to_all | solution.py:230
  15.1 1.8 %collective-permute-start.3 = (bf16[2,6,128,64]{3,2,0,1:T(8,128)(2,1)S(1)}, bf16[2,6,128,64]{3,2,0,1:T(8,128)(2,1)S(1)}, u32[]{:S(2)}, u32[]{:S(2)}) collective-permute-start(bf16[2,6,128,64]{3,2,0,1:T(8,128)(2,1)S(1)} %pad_maximum_fusion), channel_id=1, source_target_pairs={{0,1},{1,0},{2,3},{3,2},{4,5},{5,4},{6,7},{7,6},{8,9},{9,8},{10,11... | collective-permute-start | bytes 589832 | tf_op jit(solution)/shard_map/ppermute | solution.py:196
  15.2 0.7 %copy-start.8 = (s32[48]{0:T(128)S(1)}, s32[48]{0:T(128)}, u32[]{:S(2)}) copy-start(s32[48]{0:T(128)} %param.8) | copy-start | bytes 580
  17.3 9.2 %copy-start.1 = (f32[64,12,24]{2,1,0:T(8,128)S(1)}, f32[64,12,24]{2,1,0:T(8,128)}, u32[]{:S(2)}) copy-start(f32[64,12,24]{2,1,0:T(8,128)} %copy-done) | copy-start | bytes 221188
  24.9 1.6 %collective-permute-start.1 = (bf16[8,144,128]{2,1,0:T(8,128)(2,1)S(1)}, bf16[8,144,128]{2,1,0:T(8,128)(2,1)S(1)}, u32[]{:S(2)}, u32[]{:S(2)}) collective-permute-start(bf16[8,144,128]{2,1,0:T(8,128)(2,1)S(1)} %all-to-all-done.own), channel_id=1, source_target_pairs={{0,1},{1,0},{2,3},{3,2},{4,5},{5,4},{6,7},{7,6},{8,9},{9,8},{10,11... | collective-permute-start | bytes 884744 | tf_op jit(solution)/shard_map/ppermute | solution.py:196

commit v2 on v1

--- a/solution.py
+++ b/solution.py
@@ -30,30 +30,21 @@
 
 def centre_kernel(own, other, out, *, half):
     core = lax.axis_index("gz")
-    part, rows, cols = own.shape
-    total = jnp.sum(own[...], axis=0) + jnp.sum(other[...], axis=0)
-    mean = total * (1.0 / (2 * part))
-
-    def emit(first, second, base):
-        pieces = []
-        for q in range(half):
-            i = base + q
-            both = jnp.concatenate([first[:, i, :], second[:, i, :]], axis=0)
-            pieces.append(jnp.transpose(both - mean[i : i + 1, :]))
-        out[...] = jnp.concatenate(pieces, axis=0).astype(BF16)
-
-    @pl.when(core == 0)
-    def _():
-        emit(own, other, 0)
-
-    @pl.when(core == 1)
-    def _():
-        emit(other, own, half)
+    part = own.shape[2]
+    pairs = half * own.shape[1]
+    rows = pl.ds(core * half, half)
+    both = jnp.concatenate(
+        [own[rows].reshape(pairs, part), other[rows].reshape(pairs, part)], axis=1
+    )
+    both = pltpu.roll(both, core * part, 1)
+    message = (both - jnp.mean(both, axis=-1, keepdims=True)).astype(BF16)
+    for chip in range(out.shape[0]):
+        out[chip] = message
 
 
 def main_kernel(
     own, other, mask, gain_in, gain_out, wleft, wright, wgate, wout, pair, out,
-    raw, normed, left, rightt, tri, first_update, znext, right1, left1, total,
+    raw, normed, left, rightt, tri, first_update, znext, right1, left1,
     *, res, tile_rows, tile_cols, grid_rows, grid_cols,
 ):
     ch = mask.shape[1]
@@ -185,11 +176,10 @@
         ns.append(znext[at, :])
         us.append(first_update[at, :])
     gate = sigmoid(dot(jnp.concatenate(ns, axis=0), wgate[1]))
-    total[...] = jnp.concatenate(us, axis=0) + gate * dot(tn, wout[1])
+    moved = jnp.concatenate(us, axis=0) + gate * dot(tn, wout[1])
     part = ch // 2
-    for i in range(tile_rows):
-        t = pltpu.roll(total[i * tile_cols : (i + 1) * tile_cols, :], core * part, 1)
-        out[:, i, :] = pair[:, i, :] + jnp.transpose(t)[:part]
+    moved = pltpu.roll(moved, core * part, 1)[:, :part]
+    out[...] = pair[...] + moved.reshape(tile_rows, tile_cols, part)
 
 
 def swap_cores(x):
@@ -206,6 +196,7 @@
     pair, residue_mask, norm_in_gain, proj_weight, gate_weight, norm_out_gain, out_weight
 ):
     part, tile_rows, tile_cols = pair.shape
+    tile = jnp.transpose(pair, (1, 2, 0))
     grid_rows, grid_cols = lax.axis_size("gx"), lax.axis_size("gy")
     res = residue_mask.shape[0]
     ch = 2 * part
@@ -217,19 +208,18 @@
         [proj_weight, gate_weight[:, None], out_weight[:, None]], axis=1
     )
     own_gains = jnp.concatenate([norm_in_gain, norm_out_gain], axis=0)
-    other_pair = swap_cores(pair)
+    other_tile = swap_cores(tile)
     weights = join_cores(own_weights, swap_cores(own_weights), 3)
     gains = join_cores(own_gains, swap_cores(own_gains), 1)
 
+    chips = grid_rows * grid_cols
     message = pl.pallas_call(
         functools.partial(centre_kernel, half=half),
-        out_shape=jax.ShapeDtypeStruct((half * tile_cols, ch), BF16),
+        out_shape=jax.ShapeDtypeStruct((chips, half * tile_cols, ch), BF16),
+        compiler_params=pltpu.CompilerParams(vmem_limit_bytes=4 * 1024 * 1024),
         name="centre",
-    )(pair, other_pair)
-    chips = grid_rows * grid_cols
-    gathered = lax.all_to_all(
-        jnp.broadcast_to(message[None], (chips,) + message.shape), ("gx", "gy"), 0, 0
-    )
+    )(tile, other_tile)
+    gathered = lax.all_to_all(message, ("gx", "gy"), 0, 0)
     other_gathered = swap_cores(gathered)
 
     wleft = jnp.concatenate([weights[:, 0], weights[:, 1]], axis=2)
@@ -237,7 +227,7 @@
     mask = jnp.pad(residue_mask.astype(F32), (0, 8))
     mask = jnp.broadcast_to(mask[:, None], (res + 8, ch))
     vmem = lambda rows: pltpu.VMEM((rows, ch), F32)
-    return pl.pallas_call(
+    result = pl.pallas_call(
         functools.partial(
             main_kernel,
             res=res,
@@ -246,7 +236,7 @@
             grid_rows=grid_rows,
             grid_cols=grid_cols,
         ),
-        out_shape=jax.ShapeDtypeStruct(pair.shape, F32),
+        out_shape=jax.ShapeDtypeStruct(tile.shape, F32),
         scratch_shapes=[
             vmem(res * res + 8),
             vmem(res * res + 8),
@@ -257,14 +247,14 @@
             vmem(res * span),
             vmem(res * tile_cols),
             vmem(res * ipad),
-            vmem(tile_rows * tile_cols),
         ],
-        compiler_params=pltpu.CompilerParams(vmem_limit_bytes=48 * 1024 * 1024),
+        compiler_params=pltpu.CompilerParams(vmem_limit_bytes=24 * 1024 * 1024),
         name="update",
     )(
         gathered, other_gathered, mask, gains[:2], gains[2:], wleft, wright,
-        weights[:, 4], weights[:, 5], pair,
-    )
+        weights[:, 4], weights[:, 5], tile,
+    )
+    return jnp.transpose(result, (2, 0, 1))
 
 
 def layer_norm_gathered(values, gain_part):

time: 43.2 us -> 39.6 us (0.917)
  local copies, waits for them, and re-layouts: 5.68 us -> 3.57 us
  waiting for transfers between devices: 10.9 us -> 9.5 us
  Pallas kernels: 17.6 us -> 16.6 us
  other arithmetic: 0.65 us -> 1.33 us
    ppermute x4, waiting for transfers between devices: 3.35 us -> 1.6 us  [swap_cores(): return lax.ppermute(x, 'gz', [(0, 1), (1, 0)])]
    broadcast_in_dim x1 -> x0, local copies, waits for them, and re-layouts: 1.51 us -> none  [replicated(): jnp.broadcast_to(message[None], (chips,) + message.shape)]
    pallas_call x1, Pallas kernels: 2.17 us -> 0.94 us  [replicated(): pl.pallas_call(functools.partial(centre_kernel, half=half), out_shape=jax...]
    pallas_call x1 -> x0, local copies, waits for them, and re-layouts: 0.86 us -> none  [replicated(): pl.pallas_call(functools.partial(main_kernel, res=res, tile_rows=tile_row...]
    concatenate x1, other arithmetic: 0.01 us -> 0.69 us  [replicated(): own_gains = jnp.concatenate([norm_in_gain, norm_out_gain], axis=0)]
    ppermute x4, starting transfers between devices: 0.75 us -> 1.32 us  [swap_cores(): return lax.ppermute(x, 'gz', [(0, 1), (1, 0)])]
    unnamed x22 -> x15, local copies, waits for them, and re-layouts: 3.2 us -> 3.46 us
  transfers between devices with their start and end apart: 5 -> 5, of which waited for: 4 -> 3; matrix products, arithmetic and copies ran while one was open for 6% -> 7% of each run, Pallas kernels for 5% -> 2%
where the time goes in v2:
time: 39.6 us; the launch traced here: 39.2 us
  Pallas kernels  16.6 us (42%)
  waiting for transfers between devices  9.5 us (24%)
  starting transfers between devices  8.13 us (21%)
  local copies, waits for them, and re-layouts  3.57 us (9%)
  other arithmetic  1.33 us (3%)
    pallas_call x1, Pallas kernels, replicated(): pl.pallas_call(functools.partial(main_kernel, res=res, tile_rows=tile_row...  15.7 us
    all_to_all x1, waiting for transfers between devices, replicated(): gathered = lax.all_to_all(message, ('gx', 'gy'), 0, 0)  7.9 us
    all_to_all x1, starting transfers between devices, replicated(): gathered = lax.all_to_all(message, ('gx', 'gy'), 0, 0)  6.81 us
    unnamed x15, local copies, waits for them, and re-layouts  3.46 us
    ppermute x4, waiting for transfers between devices, swap_cores(): return lax.ppermute(x, 'gz', [(0, 1), (1, 0)])  1.6 us
    ppermute x4, starting transfers between devices, swap_cores(): return lax.ppermute(x, 'gz', [(0, 1), (1, 0)])  1.32 us
    pallas_call x1, Pallas kernels, replicated(): pl.pallas_call(functools.partial(centre_kernel, half=half), out_shape=jax...  0.94 us
  transfers between devices with their start and end apart: 5, of which 3 were waited for; matrix products, arithmetic and copies ran while one was open for 7% of the time, Pallas kernels for 2%

profile of v2, /device:TPU:0, one launch (start us, length us, event | category | flops | bytes accessed | tf_op | source)
XLA Modules:
  0.0 39.2 jit_solution(3045545475482999602)
XLA Ops:
  0.0 0.0 copy-start.3
  0.0 0.5 %collective-permute-start = (f32[12,24,64]{2,1,0:T(8,128)}, f32[12,24,64]{2,1,0:T(8,128)S(1)}, u32[]{:S(2)}, u32[]{:S(2)}) collective-permute-start(f32[12,24,64]{2,1,0:T(8,128)} %bitcast.16), channel_id=1, source_target_pairs={{0,1},{1,0},{2,3},{3,2},{4,5},{5,4},{6,7},{7,6},{8,9},{9,8},{10,11... | collective-permute-start | bytes 221192 | tf_op jit(solution)/shard_map/ppermute | solution.py:186
  0.5 0.2 copy-done.3
  0.7 0.7 %pad_maximum_fusion.3 = f32[4,64]{1,0:T(4,128)S(1)} fusion(f32[2,64]{1,0:T(2,128)S(1)} %copy-done.3, f32[2,64]{1,0:T(2,128)} %param.9), kind=kLoop, calls=%fused_computation.10 | loop fusion | flops 256 | bytes 2048 | tf_op jit(solution)/shard_map/concatenate | solution.py:210
  1.4 0.0 copy-start.1
  1.4 0.6 %collective-permute-start.2 = (f32[4,64]{1,0:T(4,128)S(1)}, f32[4,64]{1,0:T(4,128)S(1)}, u32[]{:S(2)}, u32[]{:S(2)}) collective-permute-start(f32[4,64]{1,0:T(4,128)S(1)} %pad_maximum_fusion.3), channel_id=1, source_target_pairs={{0,1},{1,0},{2,3},{3,2},{4,5},{5,4},{6,7},{7,6},{8,9},{9,8},{10,11... | collective-permute-start | bytes 3080 | tf_op jit(solution)/shard_map/ppermute | solution.py:186
  1.9 0.0 copy-start.2
  1.9 1.1 %copy.10 = bf16[2,4,128,64]{3,2,0,1:T(8,128)(2,1)S(1)} copy(bf16[2,4,128,64]{2,3,1,0:T(8,128)(2,1)} %param.10) | data formatting | bytes 262144 | tf_op args[3]
  3.0 0.0 copy-done.1
  3.0 0.0 copy-start
  3.0 0.1 copy.8
  3.2 0.0 copy-done.2
  3.2 0.1 copy.9
  3.3 0.0 collective-permute-done.other
  3.3 0.6 %copy-done = f32[64,12,24]{0,2,1:T(8,128)S(1)} copy-done((f32[64,12,24]{0,2,1:T(8,128)S(1)}, f32[64,12,24]{0,2,1:T(8,128)}, u32[]{:S(2)}) %copy-start) | copy-done | bytes 73752
  3.9 0.9 %centre.1 = bf16[8,144,128]{2,1,0:T(8,128)(2,1)} custom-call(f32[12,24,64]{2,1,0:T(8,128)S(1)} %bitcast.17, f32[12,24,64]{2,1,0:T(8,128)S(1)} %collective-permute-done.other), custom_call_target="tpu_custom_call" | custom-call | tf_op jit(solution)/shard_map/centre/pallas_call | solution.py:216
  4.9 6.8 %all-to-all-start = ((bf16[8,144,128]{2,1,0:T(8,128)(2,1)}), bf16[8,144,128]{2,1,0:T(8,128)(2,1)S(1)}, u32[]{:S(2)}, u32[]{:S(2)}) async-start(bf16[8,144,128]{2,1,0:T(8,128)(2,1)} %centre.1), calls=%async_computation | async-start | bytes 589824 | tf_op jit(solution)/shard_map/all_to_all | solution.py:222
  11.7 0.1 pad_maximum_fusion
  11.8 0.3 collective-permute-start.3
  12.1 0.0 copy-start.5
  12.1 0.7 %copy-done.5 = s32[48]{0:T(128)S(1)} copy-done((s32[48]{0:T(128)S(1)}, s32[48]{0:T(128)}, u32[]{:S(2)}) %copy-start.5) | copy-done | bytes 216
  12.7 0.0 copy-start.4
  12.7 0.0 collective-permute-done.2
  12.7 0.7 %copy-done.4 = f32[2,64]{1,0:T(2,128)S(1)} copy-done((f32[2,64]{1,0:T(2,128)S(1)}, f32[2,64]{1,0:T(2,128)}, u32[]{:S(2)}) %copy-start.4) | copy-done | bytes 536
  13.4 0.1 maximum_select_fusion.1
  13.5 0.1 collective-permute-done.3
  13.6 0.4 %maximum_select_fusion = bf16[2,6,128,128]{3,2,0,1:T(8,128)(2,1)S(1)} fusion(bf16[2,6,128,64]{3,2,0,1:T(8,128)(2,1)S(1)} %collective-permute-done.3, bf16[2,1,128,64]{3,2,0,1:T(8,128)(2,1)S(1)} %bitcast.22, bf16[2,1,128,64]{3,2,0,1:T(8,128)(2,1)S(1)} %bitcast.20, bf16[2,4,128,64]{3,2,0,1:T(8,128)(2,1)S(1)} %copy.10, pred[]{:T(512)S(6)} %eq.4), kind=kLoop, calls=%fused_computation.1 | loop fusion | flops 3342336 | bytes 786433 | tf_op jit(solution)/shard_map/jit(_where)/select_n | solution.py:192
  14.0 7.9 %all-to-all-done.own = bf16[8,144,128]{2,1,0:T(8,128)(2,1)S(1)} async-done(((bf16[8,144,128]{2,1,0:T(8,128)(2,1)}), bf16[8,144,128]{2,1,0:T(8,128)(2,1)S(1)}, u32[]{:S(2)}, u32[]{:S(2)}) %all-to-all-start) | async-done | bytes 294944 | tf_op jit(solution)/shard_map/all_to_all | solution.py:222
  21.9 0.0 collective-permute-start.1
  22.0 1.5 %collective-permute-done.1.other = bf16[8,144,128]{2,1,0:T(8,128)(2,1)S(1)} collective-permute-done((bf16[8,144,128]{2,1,0:T(8,128)(2,1)S(1)}, bf16[8,144,128]{2,1,0:T(8,128)(2,1)S(1)}, u32[]{:S(2)}, u32[]{:S(2)}) %collective-permute-start.1) | collective-permute-done | bytes 294944 | tf_op jit(solution)/shard_map/ppermute | solution.py:186
  23.5 0.1 broadcast_in_dim.12.mask
  23.6 15.7 %update.1 = f32[12,24,64]{2,1,0:T(8,128)} custom-call(bf16[8,144,128]{2,1,0:T(8,128)(2,1)S(1)} %all-to-all-done.own, bf16[8,144,128]{2,1,0:T(8,128)(2,1)S(1)} %collective-permute-done.1.other, f32[56,128]{1,0:T(8,128)S(1)} %broadcast_in_dim.12.mask, f32[2,128]{1,0:T(2,128)S(1)} %get-tuple-element.12.gain_in, f32[2,128]{1,0:T(2,128)S(1)} %get-tuple-element.11.gain_out, ...), custom_call_target="tpu_custom_call" | custom-call | tf_op jit(solution)/shard_map/update/pallas_call | solution.py:230
  (5 shorter events, 0.1 us)
Async XLA Ops:
  0.0 0.7 %copy-start.3 = (f32[2,64]{1,0:T(2,128)S(1)}, f32[2,64]{1,0:T(2,128)}, u32[]{:S(2)}) copy-start(f32[2,64]{1,0:T(2,128)} %param.12) | copy-start | bytes 1540
  0.0 3.3 %collective-permute-start = (f32[12,24,64]{2,1,0:T(8,128)}, f32[12,24,64]{2,1,0:T(8,128)S(1)}, u32[]{:S(2)}, u32[]{:S(2)}) collective-permute-start(f32[12,24,64]{2,1,0:T(8,128)} %bitcast.16), channel_id=1, source_target_pairs={{0,1},{1,0},{2,3},{3,2},{4,5},{5,4},{6,7},{7,6},{8,9},{9,8},{10,11... | collective-permute-start | bytes 221192 | tf_op jit(solution)/shard_map/ppermute | solution.py:186
  1.4 1.6 %copy-start.1 = (bf16[2,128,64]{1,2,0:T(8,128)(2,1)S(1)}, bf16[2,128,64]{1,2,0:T(8,128)(2,1)}, u32[]{:S(2)}) copy-start(bf16[2,128,64]{1,2,0:T(8,128)(2,1)} %param.11) | copy-start | bytes 98308
  1.4 11.4 %collective-permute-start.2 = (f32[4,64]{1,0:T(4,128)S(1)}, f32[4,64]{1,0:T(4,128)S(1)}, u32[]{:S(2)}, u32[]{:S(2)}) collective-permute-start(f32[4,64]{1,0:T(4,128)S(1)} %pad_maximum_fusion.3), channel_id=1, source_target_pairs={{0,1},{1,0},{2,3},{3,2},{4,5},{5,4},{6,7},{7,6},{8,9},{9,8},{10,11... | collective-permute-start | bytes 3080 | tf_op jit(solution)/shard_map/ppermute | solution.py:186
  1.9 1.2 %copy-start.2 = (bf16[2,128,64]{1,2,0:T(8,128)(2,1)S(1)}, bf16[2,128,64]{1,2,0:T(8,128)(2,1)}, u32[]{:S(2)}) copy-start(bf16[2,128,64]{1,2,0:T(8,128)(2,1)} %param.13) | copy-start | bytes 98308
  3.0 0.9 %copy-start = (f32[64,12,24]{0,2,1:T(8,128)S(1)}, f32[64,12,24]{0,2,1:T(8,128)}, u32[]{:S(2)}) copy-start(f32[64,12,24]{0,2,1:T(8,128)} %param.7) | copy-start | bytes 221188
  4.9 17.0 %all-to-all-start = ((bf16[8,144,128]{2,1,0:T(8,128)(2,1)}), bf16[8,144,128]{2,1,0:T(8,128)(2,1)S(1)}, u32[]{:S(2)}, u32[]{:S(2)}) async-start(bf16[8,144,128]{2,1,0:T(8,128)(2,1)} %centre.1), calls=%async_computation | async-start | bytes 589824 | tf_op jit(solution)/shard_map/all_to_all | solution.py:222
  11.8 1.8 %collective-permute-start.3 = (bf16[2,6,128,64]{3,2,0,1:T(8,128)(2,1)S(1)}, bf16[2,6,128,64]{3,2,0,1:T(8,128)(2,1)S(1)}, u32[]{:S(2)}, u32[]{:S(2)}) collective-permute-start(bf16[2,6,128,64]{3,2,0,1:T(8,128)(2,1)S(1)} %pad_maximum_fusion), channel_id=1, source_target_pairs={{0,1},{1,0},{2,3},{3,2},{4,5},{5,4},{6,7},{7,6},{8,9},{9,8},{10,11... | collective-permute-start | bytes 589832 | tf_op jit(solution)/shard_map/ppermute | solution.py:186
  12.1 0.7 %copy-start.5 = (s32[48]{0:T(128)S(1)}, s32[48]{0:T(128)}, u32[]{:S(2)}) copy-start(s32[48]{0:T(128)} %param.8) | copy-start | bytes 580
  12.7 0.7 %copy-start.4 = (f32[2,64]{1,0:T(2,128)S(1)}, f32[2,64]{1,0:T(2,128)}, u32[]{:S(2)}) copy-start(f32[2,64]{1,0:T(2,128)} %param.9) | copy-start | bytes 1540
  21.9 1.6 %collective-permute-start.1 = (bf16[8,144,128]{2,1,0:T(8,128)(2,1)S(1)}, bf16[8,144,128]{2,1,0:T(8,128)(2,1)S(1)}, u32[]{:S(2)}, u32[]{:S(2)}) collective-permute-start(bf16[8,144,128]{2,1,0:T(8,128)(2,1)S(1)} %all-to-all-done.own), channel_id=1, source_target_pairs={{0,1},{1,0},{2,3},{3,2},{4,5},{5,4},{6,7},{7,6},{8,9},{9,8},{10,11... | collective-permute-start | bytes 884744 | tf_op jit(solution)/shard_map/ppermute | solution.py:186

commit v3 on v0

--- a/solution.py
+++ b/solution.py
@@ -1,9 +1,308 @@
+import functools
+
 import jax
 import jax.numpy as jnp
 from jax import lax
+from jax.experimental import pallas as pl
+from jax.experimental.pallas import tpu as pltpu
 from jax.sharding import PartitionSpec as P
 
 EPSILON = 1e-05
+F32 = jnp.float32
+BF16 = jnp.bfloat16
+REPLICATED_LIMIT = 4 * 1024 * 1024
+
+
+def dot(x, w):
+    return jnp.dot(x.astype(BF16), w, preferred_element_type=F32)
+
+
+def lane_norm(x, gain, ones):
+    d = x - jnp.mean(x, axis=-1, keepdims=True)
+    return d * lax.rsqrt(dot(d * d, ones) + EPSILON) * gain
+
+
+def gated(x, w):
+    p = dot(x, w)
+    ch = p.shape[1] // 2
+    return (jnp.tanh(p[:, :ch]) + 1.0) * p[:, ch:]
+
+
+def steps(total, size, body, unrolled=False):
+    if unrolled or size >= total:
+        for first in range(0, total, size):
+            body(first)
+    else:
+
+        def step(n, carry):
+            body(pl.multiple_of(n * size, size))
+            return carry
+
+        lax.fori_loop(0, total // size, step, 0)
+
+
+def rows_at(first, count):
+    return pl.ds(first if isinstance(first, int) else pl.multiple_of(first, 8), count)
+
+
+def centre_kernel(own, other, out, *, half):
+    core = lax.axis_index("gz")
+    part = own.shape[2]
+    pairs = half * own.shape[1]
+    rows = pl.ds(core * half, half)
+    both = jnp.concatenate(
+        [own[rows].reshape(pairs, part), other[rows].reshape(pairs, part)], axis=1
+    )
+    both = pltpu.roll(both, core * part, 1)
+    message = (both - jnp.mean(both, axis=-1, keepdims=True)).astype(BF16)
+    for chip in range(out.shape[0]):
+        out[chip] = message
+
+
+def weights_kernel(own, other, own_gains, other_gains, flags, wleft, wright, wgate, wout, gains, mask):
+    core = lax.axis_index("gz")
+    half = own.shape[2]
+    for u in range(2):
+        for p in range(6):
+            mine, theirs = own[u, p].astype(F32) * 0.5, other[u, p].astype(F32) * 0.5
+            first = jnp.where(core == 0, mine, theirs)
+            second = jnp.where(core == 0, theirs, mine)
+            full = jnp.transpose(jnp.concatenate([first, second], axis=0)).astype(BF16)
+            if p < 2:
+                wleft[u, :, p * 2 * half : (p + 1) * 2 * half] = full
+            elif p < 4:
+                wright[u, :, (p - 2) * 2 * half : (p - 1) * 2 * half] = full
+            elif p == 4:
+                wgate[u] = full
+            else:
+                wout[u] = full
+    gains[...] = pltpu.roll(jnp.concatenate([own_gains[...], other_gains[...]], axis=1), core * half, 1)
+    row = flags[...].astype(F32)
+    size = row.shape[1]
+    wide = jnp.transpose(jnp.broadcast_to(row, (mask.shape[1], size)))
+    mask[...] = jnp.zeros_like(mask)
+    mask[:size, :] = wide
+
+
+def main_kernel(
+    own, other, mask, gains, wleft, wright, wgate, wout, pair, out,
+    raw, normed, left, rightt, tri, first_update, znext, right1, left1,
+    *, res, tile_rows, tile_cols, grid_rows, grid_cols, sizes,
+):
+    ch = mask.shape[1]
+    half = tile_rows // 2
+    ipad = -(-tile_rows // 8) * 8
+    span = tile_cols + ipad
+    row_block = lax.axis_index("gx")
+    col_block = lax.axis_index("gy")
+    core = lax.axis_index("gz")
+    first_col = col_block * tile_cols
+    first_row = row_block * tile_rows
+    ones = jnp.full((ch, ch), 1.0 / ch, BF16)
+    gain_in, gain_out = gains[0:2, :], gains[2:4, :]
+
+    def norm_block(block):
+        for n in range(sizes["norm"]):
+            at_block = block + n
+            for source, which in ((own, core), (other, 1 - core)):
+                x = source[at_block].astype(F32)
+                var = jnp.mean(x * x, axis=-1, keepdims=True)
+                zn = x * lax.rsqrt(var + EPSILON) * gain_in[0:1]
+                base = (at_block // grid_cols * tile_rows + which * half) * res
+                base = base + at_block % grid_cols * tile_cols
+                for q in range(half):
+                    at = pl.ds(pl.multiple_of(base + q * res, 8), tile_cols)
+                    raw[at, :] = x[q * tile_cols : (q + 1) * tile_cols]
+                    normed[at, :] = zn[q * tile_cols : (q + 1) * tile_cols]
+
+    steps(grid_rows * grid_cols, sizes["norm"], norm_block)
+    raw[pl.ds(res * res, 8), :] = jnp.zeros((8, ch), F32)
+    normed[pl.ds(res * res, 8), :] = jnp.zeros((8, ch), F32)
+
+    def left_block(first):
+        count = sizes["left"]
+        at = rows_at(first * res, count * res)
+        y = gated(normed[at, :], wleft[0]).reshape(count, res, ch) * mask[:res, :][None]
+        left[at, :] = y.reshape(count * res, ch)
+
+    steps(res, sizes["left"], left_block)
+
+    for k in range(ipad - tile_rows):
+        rightt[pl.ds(tile_cols + tile_rows + k, res, stride=span), :] = jnp.zeros((res, ch), F32)
+
+    def right_block(slot):
+        count = sizes["right"]
+        row = first_col + slot if slot < tile_cols else first_row + slot - tile_cols
+        y = gated(normed[rows_at(row * res, count * res), :], wright[0])
+        for q in range(count):
+            rightt[pl.ds(slot + q, res, stride=span), :] = y[q * res : (q + 1) * res]
+
+    steps(tile_cols + tile_rows, sizes["right"], right_block, unrolled=True)
+
+    def tri_block(first):
+        count = sizes["tri"]
+
+        def add(k, accs):
+            r = rightt[pl.ds(pl.multiple_of(k * span, 8), span), :]
+            return tuple(acc + left[pl.ds((first + q) * res + k, 1), :] * r for q, acc in enumerate(accs))
+
+        accs = lax.fori_loop(
+            0, res, add, tuple(jnp.zeros((span, ch), F32) for _ in range(count)), unroll=sizes["unroll"]
+        )
+        for q in range(count):
+            tri[rows_at((first + q) * span, span), :] = accs[q]
+
+    steps(res, sizes["tri"], tri_block)
+
+    smask = jnp.concatenate(
+        [mask[rows_at(first_col, tile_cols), :], mask[pl.ds(first_row, ipad), :]], axis=0
+    )
+
+    def out_block(first):
+        count = sizes["out"]
+        zs, ns, ms = [], [], []
+        for q in range(count):
+            r = first + q
+            at_cols = pl.ds(pl.multiple_of(r * res + first_col, 8), tile_cols)
+            at_rows = pl.ds(r * res + first_row, ipad)
+            zs += [raw[at_cols, :], raw[at_rows, :]]
+            ns += [normed[at_cols, :], normed[at_rows, :]]
+            ms.append(smask * mask[pl.ds(r, 1), :])
+        at = rows_at(first * span, count * span)
+        gate = jnp.tanh(dot(jnp.concatenate(ns, axis=0), wgate[0])) + 1.0
+        tn = lane_norm(tri[at, :], gain_out[0:1], ones)
+        update = gate * dot(tn, wout[0]) * jnp.concatenate(ms, axis=0)
+        first_update[at, :] = update
+        znext[at, :] = lane_norm(jnp.concatenate(zs, axis=0) + update, gain_in[1:2], ones)
+
+    steps(res, sizes["out"], out_block)
+
+    def second_block(first):
+        count = sizes["second"]
+        rs, ls = [], []
+        for q in range(count):
+            at = (first + q) * span
+            rs.append(znext[rows_at(at, tile_cols), :])
+            ls.append(znext[rows_at(at + tile_cols, ipad), :])
+        rows = mask[rows_at(first, count), :]
+        at = rows_at(first * tile_cols, count * tile_cols)
+        right1[at, :] = gated(jnp.concatenate(rs, axis=0), wright[1])
+        v = gated(jnp.concatenate(ls, axis=0), wleft[1]).reshape(count, ipad, ch) * rows[:, None, :]
+        left1[rows_at(first * ipad, count * ipad), :] = v.reshape(count * ipad, ch)
+
+    steps(res, sizes["second"], second_block)
+
+    def tri1_block(k, accs):
+        r = right1[pl.ds(pl.multiple_of(k * tile_cols, 8), tile_cols), :]
+        return tuple(acc + left1[pl.ds(k * ipad + i, 1), :] * r for i, acc in enumerate(accs))
+
+    accs = lax.fori_loop(
+        0, res, tri1_block, tuple(jnp.zeros((tile_cols, ch), F32) for _ in range(tile_rows)), unroll=4
+    )
+    tn = lane_norm(jnp.concatenate(accs, axis=0), gain_out[1:2], ones)
+    ns, us, ms = [], [], []
+    for i in range(tile_rows):
+        at = pl.ds(pl.multiple_of((first_row + i) * span, 8), tile_cols)
+        ns.append(znext[at, :])
+        us.append(first_update[at, :])
+        ms.append(smask[:tile_cols] * mask[pl.ds(first_row + i, 1), :])
+    gate = jnp.tanh(dot(jnp.concatenate(ns, axis=0), wgate[1])) + 1.0
+    update = gate * dot(tn, wout[1]) * jnp.concatenate(ms, axis=0)
+    moved = jnp.concatenate(us, axis=0) + update
+    part = ch // 2
+    moved = pltpu.roll(moved, core * part, 1)[:, :part]
+    out[...] = pair[...] + moved.reshape(tile_rows, tile_cols, part)
+
+
+def swap_cores(x):
+    return lax.ppermute(x, "gz", [(0, 1), (1, 0)])
+
+
+def replicated(
+    pair, residue_mask, norm_in_gain, proj_weight, gate_weight, norm_out_gain, out_weight
+):
+    part, tile_rows, tile_cols = pair.shape
+    tile = jnp.transpose(pair, (1, 2, 0))
+    grid_rows, grid_cols = lax.axis_size("gx"), lax.axis_size("gy")
+    res = residue_mask.shape[0]
+    ch = 2 * part
+    half = tile_rows // 2
+    ipad = -(-tile_rows // 8) * 8
+    span = tile_cols + ipad
+
+    other_tile = swap_cores(tile)
+    chips = grid_rows * grid_cols
+    message = pl.pallas_call(
+        functools.partial(centre_kernel, half=half),
+        out_shape=jax.ShapeDtypeStruct((chips, half * tile_cols, ch), BF16),
+        compiler_params=pltpu.CompilerParams(vmem_limit_bytes=4 * 1024 * 1024),
+        name="centre",
+    )(tile, other_tile)
+    own_weights = jnp.concatenate(
+        [
+            jnp.transpose(proj_weight, (0, 1, 3, 2)),
+            jnp.transpose(gate_weight, (0, 2, 1))[:, None],
+            jnp.transpose(out_weight, (0, 2, 1))[:, None],
+        ],
+        axis=1,
+    )
+    own_gains = jnp.concatenate([norm_in_gain, norm_out_gain], axis=0)
+    gathered = lax.all_to_all(message, ("gx", "gy"), 0, 0)
+    wleft, wright, wgate, wout, gains, mask = pl.pallas_call(
+        weights_kernel,
+        out_shape=[
+            jax.ShapeDtypeStruct((2, ch, 2 * ch), BF16),
+            jax.ShapeDtypeStruct((2, ch, 2 * ch), BF16),
+            jax.ShapeDtypeStruct((2, ch, ch), BF16),
+            jax.ShapeDtypeStruct((2, ch, ch), BF16),
+            jax.ShapeDtypeStruct((4, ch), F32),
+            jax.ShapeDtypeStruct((res + 8, ch), F32),
+        ],
+        compiler_params=pltpu.CompilerParams(vmem_limit_bytes=8 * 1024 * 1024),
+        cost_estimate=pl.CostEstimate(flops=2**24, bytes_accessed=2**20, transcendentals=0),
+        name="weights",
+    )(own_weights, swap_cores(own_weights), own_gains, swap_cores(own_gains), residue_mask[None, :])
+    other_gathered = swap_cores(gathered)
+
+    def fitting(total, size):
+        return size if total % size == 0 else next(n for n in (8, 4, 2, 1) if total % n == 0)
+
+    sizes = {
+        "norm": chips,
+        "left": res,
+        "right": fitting(tile_rows, 12) if tile_cols % 12 == 0 else 4,
+        "tri": fitting(res, 4),
+        "unroll": fitting(res, 24),
+        "out": res,
+        "second": res,
+    }
+    vmem = lambda rows: pltpu.VMEM((rows, ch), F32)
+    result = pl.pallas_call(
+        functools.partial(
+            main_kernel,
+            res=res,
+            tile_rows=tile_rows,
+            tile_cols=tile_cols,
+            grid_rows=grid_rows,
+            grid_cols=grid_cols,
+            sizes=sizes,
+        ),
+        out_shape=jax.ShapeDtypeStruct(tile.shape, F32),
+        scratch_shapes=[
+            vmem(res * res + 8),
+            vmem(res * res + 8),
+            vmem(res * res),
+            vmem(res * span),
+            vmem(res * span),
+            vmem(res * span),
+            vmem(res * span),
+            vmem(res * tile_cols),
+            vmem(res * ipad),
+        ],
+        compiler_params=pltpu.CompilerParams(vmem_limit_bytes=24 * 1024 * 1024),
+        name="update",
+    )(gathered, other_gathered, mask, gains, wleft, wright, wgate, wout, tile)
+    return jnp.transpose(result, (2, 0, 1))
 
 
 def layer_norm_gathered(values, gain_part):
@@ -46,7 +345,7 @@
     )
 
 
-def per_device(
+def distributed(
     pair, residue_mask, norm_in_gain, proj_weight, gate_weight, norm_out_gain, out_weight
 ):
     tile_rows = pair.shape[1]
@@ -80,6 +379,23 @@
     return current
 
 
+def fits_replicated(pair, residue_mask):
+    part, tile_rows, tile_cols = pair.shape
+    res = residue_mask.shape[0]
+    return (
+        lax.axis_size("gz") == 2
+        and res * res * part * 2 * 4 <= REPLICATED_LIMIT
+        and res % 8 == 0
+        and tile_rows % 4 == 0
+        and tile_cols % 8 == 0
+    )
+
+
+def per_device(pair, residue_mask, *parameters):
+    plan = replicated if fits_replicated(pair, residue_mask) else distributed
+    return plan(pair, residue_mask, *parameters)
+
+
 def solution(mesh):
     return jax.shard_map(
         per_device,

time: 110 us -> 31.2 us (0.28)
  blocking collectives: 84.3 us -> 17.7 us
  local copies, waits for them, and re-layouts: 12.3 us -> 1.55 us
  Pallas kernels: 0 us -> 7.92 us
  starting transfers between devices: 6.52 us -> 1.61 us
  matrix products: 3.03 us -> 0 us
  waiting for transfers between devices: 0.01 us -> 2.04 us
  other arithmetic: 1.82 us -> 0.04 us
    all_gather x8 -> x0, blocking collectives: 48.2 us -> none  [the longest x2 27.9 us: fold_panels(): lax.all_gather(right_tile, 'gx', axis=1, tiled=True)]
    all_to_all x4 -> x1, blocking collectives: 33.6 us -> 17.7 us  [replicated(): gathered = lax.all_to_all(message, ('gx', 'gy'), 0, 0)]
    pallas_call x0 -> x3, Pallas kernels: none -> 7.92 us  [the longest x1 7.33 us: replicated(): pl.pallas_call(functools.partial(main_kernel, res=res, tile_rows=tile_row...]
    unnamed x42 -> x16, local copies, waits for them, and re-layouts: 8.64 us -> 1.55 us
    all_to_all x2 -> x0, starting transfers between devices: 6.52 us -> none  [transpose_tile(): lax.all_to_all(lax.all_to_all(blocks, 'gx', split_axis=2, concat_axis=2,...]
    all_gather x8 -> x0, local copies, waits for them, and re-layouts: 3.05 us -> none  [the longest x4 1.32 us: layer_norm_gathered(): lax.all_gather(values, 'gz', axis=0, tiled=True)]
    dot_general x8 -> x0, matrix products: 3.03 us -> none  [the longest x2 1.25 us: per_device(): jnp.einsum('cij,cd->dij', normed, gate_weight[update], preferred_element_...]
    unnamed x1 -> x0, blocking collectives: 2.48 us -> none
  transfers between devices with their start and end apart: 2 -> 4, of which waited for: 0 -> 2; matrix products, arithmetic and copies ran while one was open for 1% -> 0% of each run, Pallas kernels for 0% -> 1%
where the time goes in v3:
time: 31.2 us; the launch traced here: 31 us
  blocking collectives  17.7 us (57%)
  Pallas kernels  7.92 us (25%)
  waiting for transfers between devices  2.04 us (7%)
  starting transfers between devices  1.61 us (5%)
  local copies, waits for them, and re-layouts  1.55 us (5%)
    all_to_all x1, blocking collectives, replicated(): gathered = lax.all_to_all(message, ('gx', 'gy'), 0, 0)  17.7 us
    pallas_call x1, Pallas kernels, replicated(): pl.pallas_call(functools.partial(main_kernel, res=res, tile_rows=tile_row...  7.33 us
    ppermute x4, waiting for transfers between devices, swap_cores(): return lax.ppermute(x, 'gz', [(0, 1), (1, 0)])  2.04 us
    ppermute x4, starting transfers between devices, swap_cores(): return lax.ppermute(x, 'gz', [(0, 1), (1, 0)])  1.61 us
    unnamed x16, local copies, waits for them, and re-layouts  1.55 us
  transfers between devices with their start and end apart: 4, of which 2 were waited for; matrix products, arithmetic and copies ran while one was open for 0% of the time, Pallas kernels for 1%

profile of v3, /device:TPU:0, one launch (start us, length us, event | category | flops | bytes accessed | tf_op | source)
XLA Modules:
  0.0 31.0 jit_solution(5386781604986870243)
XLA Ops:
  0.0 0.5 %collective-permute-start = (f32[12,24,64]{2,1,0:T(8,128)}, f32[12,24,64]{2,1,0:T(8,128)S(1)}, u32[]{:S(2)}, u32[]{:S(2)}) collective-permute-start(f32[12,24,64]{2,1,0:T(8,128)} %bitcast.10), channel_id=1, source_target_pairs={{0,1},{1,0},{2,3},{3,2},{4,5},{5,4},{6,7},{7,6},{8,9},{9,8},{10,11... | collective-permute-start | bytes 221192 | tf_op jit(solution)/shard_map/ppermute | solution.py:218
  0.5 1.2 %collective-permute-done.other = f32[12,24,64]{2,1,0:T(8,128)S(1)} collective-permute-done((f32[12,24,64]{2,1,0:T(8,128)}, f32[12,24,64]{2,1,0:T(8,128)S(1)}, u32[]{:S(2)}, u32[]{:S(2)}) %collective-permute-start) | collective-permute-done | bytes 73760 | tf_op jit(solution)/shard_map/ppermute | solution.py:218
  1.7 0.0 copy-start
  1.7 0.9 %copy-done = f32[64,12,24]{0,2,1:T(8,128)S(1)} copy-done((f32[64,12,24]{0,2,1:T(8,128)S(1)}, f32[64,12,24]{0,2,1:T(8,128)}, u32[]{:S(2)}) %copy-start) | copy-done | bytes 73752
  2.6 0.2 centre.1
  2.9 0.0 copy-start.3
  2.9 0.0 copy-start.4
  2.9 0.0 copy-start.5
  2.9 17.7 %all_to_all.5.own = bf16[8,144,128]{2,1,0:T(8,128)(2,1)S(1)} all-to-all(bf16[8,144,128]{2,1,0:T(8,128)(2,1)S(1)} %centre.1), channel_id=1, replica_groups=mesh['groups'=2,'gx'=4,'gy'=2,'gz'=2] {'gx','gy'}, dimensions={0} | all-to-all | bytes 589824 | tf_op jit(solution)/shard_map/all_to_all | solution.py:250
  20.6 0.0 collective-permute-start.1
  20.6 0.0 copy-done.3
  20.6 0.0 copy-done.4
  20.6 0.0 copy-done.5
  20.7 0.0 copy-start.6
  20.7 0.0 copy-start.7
  20.7 0.6 %collective-permute-start.2 = (bf16[2,6,64,128]{3,2,1,0:T(8,128)(2,1)S(1)}, bf16[2,6,64,128]{3,2,1,0:T(8,128)(2,1)S(1)}, u32[]{:S(2)}, u32[]{:S(2)}) collective-permute-start(bf16[2,6,64,128]{3,2,1,0:T(8,128)(2,1)S(1)} %pad_maximum_fusion.own), channel_id=1, source_target_pairs={{0,1},{1,0},{2,3},{3,2},{4,5},{5,4},{6,7},{7,6},{8,9},{9,8},{10,11... | collective-permute-start | bytes 589832 | tf_op jit(solution)/shard_map/ppermute | solution.py:218
  21.3 0.1 copy-done.6
  21.3 0.0 copy-done.7
  21.4 0.0 copy-start.2
  21.4 0.6 %collective-permute-start.3 = (f32[4,64]{1,0:T(4,128)S(1)}, f32[4,64]{1,0:T(4,128)S(1)}, u32[]{:S(2)}, u32[]{:S(2)}) collective-permute-start(f32[4,64]{1,0:T(4,128)S(1)} %pad_maximum_fusion.1.own_gains), channel_id=1, source_target_pairs={{0,1},{1,0},{2,3},{3,2},{4,5},{5,4},{6,7},{7,6},{8,9},{9,8},{10,11... | collective-permute-start | bytes 3080 | tf_op jit(solution)/shard_map/ppermute | solution.py:218
  21.9 0.8 %collective-permute-done.3.other_gains = f32[4,64]{1,0:T(4,128)S(1)} collective-permute-done((f32[4,64]{1,0:T(4,128)S(1)}, f32[4,64]{1,0:T(4,128)S(1)}, u32[]{:S(2)}, u32[]{:S(2)}) %collective-permute-start.3) | collective-permute-done | bytes 1056 | tf_op jit(solution)/shard_map/ppermute | solution.py:218
  22.7 0.0 collective-permute-done.2.other
  22.8 0.0 copy-done.2
  22.8 0.0 copy-start.1
  22.8 0.4 %weights.1 = (bf16[2,128,256]{2,1,0:T(8,128)(2,1)S(1)}, bf16[2,128,256]{2,1,0:T(8,128)(2,1)S(1)}, bf16[2,128,128]{2,1,0:T(8,128)(2,1)S(1)}, bf16[2,128,128]{2,1,...) custom-call(bf16[2,6,64,128]{3,2,1,0:T(8,128)(2,1)S(1)} %pad_maximum_fusion.own, ...), custom_call_target="tpu_custom_call" | custom-call | flops 16777216 | bytes 1048576 | tf_op jit(solution)/shard_map/weights/pallas_call | solution.py:251
  23.1 0.0 collective-permute-done.1.other
  23.1 0.5 %copy-done.1 = f32[64,12,24]{0,2,1:T(8,128)S(1)} copy-done((f32[64,12,24]{0,2,1:T(8,128)S(1)}, f32[64,12,24]{0,2,1:T(8,128)}, u32[]{:S(2)}) %copy-start.1) | copy-done | bytes 73752
  23.7 7.3 %update.1 = f32[12,24,64]{2,1,0:T(8,128)} custom-call(bf16[8,144,128]{2,1,0:T(8,128)(2,1)S(1)} %all_to_all.5.own, bf16[8,144,128]{2,1,0:T(8,128)(2,1)S(1)} %collective-permute-done.1.other, f32[56,128]{1,0:T(8,128)S(1)} %get-tuple-element.11.mask, f32[4,128]{1,0:T(4,128)S(1)} %get-tuple-element.12.gains, bf16[2,128,256]{2,1,0:T(8,128)(2,1)S(1)} %get-tuple-element.13.wleft, ...), custom_call_target="tpu_custom_call" | custom-call | tf_op jit(solution)/shard_map/update/pallas_call | solution.py:280
  (2 shorter events, 0.0 us)
Async XLA Ops:
  0.0 1.7 %collective-permute-start = (f32[12,24,64]{2,1,0:T(8,128)}, f32[12,24,64]{2,1,0:T(8,128)S(1)}, u32[]{:S(2)}, u32[]{:S(2)}) collective-permute-start(f32[12,24,64]{2,1,0:T(8,128)} %bitcast.10), channel_id=1, source_target_pairs={{0,1},{1,0},{2,3},{3,2},{4,5},{5,4},{6,7},{7,6},{8,9},{9,8},{10,11... | collective-permute-start | bytes 221192 | tf_op jit(solution)/shard_map/ppermute | solution.py:218
  1.7 0.9 %copy-start = (f32[64,12,24]{0,2,1:T(8,128)S(1)}, f32[64,12,24]{0,2,1:T(8,128)}, u32[]{:S(2)}) copy-start(f32[64,12,24]{0,2,1:T(8,128)} %param.7) | copy-start | bytes 221188
  2.9 17.8 %copy-start.3 = (bf16[2,4,128,64]{2,3,1,0:T(8,128)(2,1)S(1)}, bf16[2,4,128,64]{2,3,1,0:T(8,128)(2,1)}, u32[]{:S(2)}) copy-start(bf16[2,4,128,64]{2,3,1,0:T(8,128)(2,1)} %param.10) | copy-start | bytes 393220
  2.9 17.8 %copy-start.4 = (bf16[2,128,64]{1,2,0:T(8,128)(2,1)S(1)}, bf16[2,128,64]{1,2,0:T(8,128)(2,1)}, u32[]{:S(2)}) copy-start(bf16[2,128,64]{1,2,0:T(8,128)(2,1)} %param.13) | copy-start | bytes 98308
  2.9 17.8 %copy-start.5 = (bf16[2,128,64]{1,2,0:T(8,128)(2,1)S(1)}, bf16[2,128,64]{1,2,0:T(8,128)(2,1)}, u32[]{:S(2)}) copy-start(bf16[2,128,64]{1,2,0:T(8,128)(2,1)} %param.11) | copy-start | bytes 98308
  20.6 2.5 %collective-permute-start.1 = (bf16[8,144,128]{2,1,0:T(8,128)(2,1)S(1)}, bf16[8,144,128]{2,1,0:T(8,128)(2,1)S(1)}, u32[]{:S(2)}, u32[]{:S(2)}) collective-permute-start(bf16[8,144,128]{2,1,0:T(8,128)(2,1)S(1)} %all_to_all.5.own), channel_id=1, source_target_pairs={{0,1},{1,0},{2,3},{3,2},{4,5},{5,4},{6,7},{7,6},{8,9},{9,8},{10,11... | collective-permute-start | bytes 884744 | tf_op jit(solution)/shard_map/ppermute | solution.py:218
  20.7 0.7 %copy-start.6 = (f32[2,64]{1,0:T(2,128)S(1)}, f32[2,64]{1,0:T(2,128)}, u32[]{:S(2)}) copy-start(f32[2,64]{1,0:T(2,128)} %param.12) | copy-start | bytes 1540
  20.7 0.7 %copy-start.7 = (f32[2,64]{1,0:T(2,128)S(1)}, f32[2,64]{1,0:T(2,128)}, u32[]{:S(2)}) copy-start(f32[2,64]{1,0:T(2,128)} %param.9) | copy-start | bytes 1540
  20.7 2.0 %collective-permute-start.2 = (bf16[2,6,64,128]{3,2,1,0:T(8,128)(2,1)S(1)}, bf16[2,6,64,128]{3,2,1,0:T(8,128)(2,1)S(1)}, u32[]{:S(2)}, u32[]{:S(2)}) collective-permute-start(bf16[2,6,64,128]{3,2,1,0:T(8,128)(2,1)S(1)} %pad_maximum_fusion.own), channel_id=1, source_target_pairs={{0,1},{1,0},{2,3},{3,2},{4,5},{5,4},{6,7},{7,6},{8,9},{9,8},{10,11... | collective-permute-start | bytes 589832 | tf_op jit(solution)/shard_map/ppermute | solution.py:218
  21.4 1.4 %copy-start.2 = (s32[48]{0:T(128)S(1)}, s32[48]{0:T(128)}, u32[]{:S(2)}) copy-start(s32[48]{0:T(128)} %param.8) | copy-start | bytes 580
  21.4 1.4 %collective-permute-start.3 = (f32[4,64]{1,0:T(4,128)S(1)}, f32[4,64]{1,0:T(4,128)S(1)}, u32[]{:S(2)}, u32[]{:S(2)}) collective-permute-start(f32[4,64]{1,0:T(4,128)S(1)} %pad_maximum_fusion.1.own_gains), channel_id=1, source_target_pairs={{0,1},{1,0},{2,3},{3,2},{4,5},{5,4},{6,7},{7,6},{8,9},{9,8},{10,11... | collective-permute-start | bytes 3080 | tf_op jit(solution)/shard_map/ppermute | solution.py:218
  22.8 0.9 %copy-start.1 = (f32[64,12,24]{0,2,1:T(8,128)S(1)}, f32[64,12,24]{0,2,1:T(8,128)}, u32[]{:S(2)}) copy-start(f32[64,12,24]{0,2,1:T(8,128)} %param.7) | copy-start | bytes 221188
